TPU v7x, 32 devices: a whole 2x2x4 slice. The times are simulated.
32 devices in a mesh: rows: 4 (over y, x), wide: 8 (over z, core).
Axes of the slice: x: 2, y: 2, z: 4, core: 2. Of those that a mesh axis runs over, the one named last changes fastest.
Arguments:
- tokens: bfloat16 [16, 1024, 1024], P('rows', 'wide'), may hold values from -6 to 6
- segments: int32 [16, 1024], P('rows'), may hold values from 0 to 15, never falling along the last dimension, each value on 1 to 128 neighbouring positions
- w_qkv: bfloat16 [2, 1024, 3072], replicated, may hold values from -0.1875 to 0.1875
- b_qkv: float32 [2, 3072], replicated, may hold values from -3 to 3
- w_out: bfloat16 [2, 1024, 1024], replicated, may hold values from -1 to 1
- b_out: float32 [2, 1024], replicated, may hold values from -3 to 3
- norm_gain: float32 [2, 2, 1024], replicated, may hold values from 0.5 to 1.5
- norm_bias: float32 [2, 2, 1024], replicated, may hold values from -2 to 2
- w_up: bfloat16 [2, 4096, 1024], P(None, 'wide'), may hold values from -0.1875 to 0.1875
- b_up: bfloat16 [2, 4096], P(None, 'wide'), may hold values from -3 to 3
- w_down: bfloat16 [2, 4096, 1024], P(None, 'wide'), may hold values from -0.09375 to 0.09375
- b_down: float32 [2, 1024], replicated, may hold values from -2 to 2
- prefix: bfloat16 [2, 2, 64, 1024], replicated, may hold values from -6 to 6
- cotangent: bfloat16 [16, 1024, 1024], P('rows', 'wide'), may hold values from -6 to 6
Outputs:
- output: bfloat16 [16, 1024, 1024], P('rows', 'wide')
- grad_tokens: float32 [16, 1024, 1024], P('rows', 'wide')
- grad_prefix: float32 [2, 2, 64, 1024], replicated
Inputs may be any that keep to these rules, and one draw needn't show every extreme that they name: `segments`: along each row the pair ids never fall, each pair covers 1 to 128 consecutive positions, and some pair covers exactly 128.
All inputs are finite; a program needn't handle non-finite values.
Results may differ from a plain program's by a relative error of at most 0.02.
Values may be sent and summed in bfloat16 or wider, within the bound.
A program may use at most 320 MiB of HBM per device.

v0:
```python
import math
import jax
import jax.numpy as jnp
from jax import lax
from jax.sharding import PartitionSpec as P

HEADS = 16
PAIR_MAX = 128
LAYERS = 2


def extended(block, sides, width):
    for axis, dim in sides:
        count = lax.axis_size(axis)
        forward = [(i, i + 1) for i in range(count - 1)]
        backward = [(target, source) for source, target in forward]
        low = lax.ppermute(
            lax.slice_in_dim(block, block.shape[dim] - width, None, axis=dim), axis, forward
        )
        high = lax.ppermute(lax.slice_in_dim(block, 0, width, axis=dim), axis, backward)
        block = jnp.concatenate([low, block, high], axis=dim)
    return block


def normalize(values, gain, shift):
    center = values - jnp.mean(values, axis=-1, keepdims=True)
    spread = jnp.mean(center * center, axis=-1, keepdims=True)
    return center * lax.rsqrt(spread + 1e-05) * gain + shift


def gelu_exact(values):
    return jax.nn.gelu(values, approximate=False)


def gelu_back(pre_values, grad_values):
    return jax.vjp(gelu_exact, pre_values)[1](grad_values)[0]


def norm_grad(values, gain, shift, grad_values):
    return jax.vjp(lambda inner: normalize(inner, gain, shift), values)[1](grad_values)[0]


def multiply(left, right):
    return jnp.dot(left, right, preferred_element_type=jnp.float32)


def multiply_back(left, right):
    return lax.dot_general(
        left, right, (((1,), (1,)), ((), ())), preferred_element_type=jnp.float32
    )


def local(
    tokens,
    segments,
    w_qkv,
    b_qkv,
    w_out,
    b_out,
    norm_gain,
    norm_bias,
    w_up,
    b_up,
    w_down,
    b_down,
    prefix,
    cotangent,
):
    seqs_here, tok_here, model_width = tokens.shape
    rows_here = seqs_here * tok_here
    head_count = HEADS
    head_size = model_width // head_count
    score_scale = 1.0 / math.sqrt(head_size)
    rim_rows = PAIR_MAX
    prefix_len = prefix.shape[2]
    position = lax.axis_index("wide") * tok_here
    padded_ids = jnp.pad(segments, ((0, 0), (rim_rows, rim_rows)), constant_values=-1)
    query_ids = lax.dynamic_slice_in_dim(segments, position, tok_here, 1)
    window_ids = lax.dynamic_slice_in_dim(padded_ids, position, tok_here + 2 * rim_rows, 1)
    prefix_mask = jnp.ones((seqs_here, prefix_len, tok_here), dtype=bool)
    visible = jnp.concatenate(
        [prefix_mask, window_ids[:, :, None] == query_ids[:, None, :]], axis=1
    )[:, None]

    def split_heads(values):
        return values.reshape(seqs_here, values.shape[1], head_count, head_size)

    def with_prefix(layer_index, member, window_part):
        fixed_rows = jnp.broadcast_to(
            prefix[layer_index, member][None], (seqs_here, prefix_len, model_width)
        )
        return split_heads(jnp.concatenate([fixed_rows, window_part], axis=1))

    def score_block(queries, key_all):
        scores = (
            jnp.einsum("sqhe,skhe->shkq", queries, key_all, preferred_element_type=jnp.float32)
            * score_scale
        )
        return jnp.where(visible, scores, -1e30)

    hidden = tokens.astype(jnp.float32).reshape(rows_here, model_width)
    stored = []
    for layer_index in range(LAYERS):
        qkv_all = multiply(hidden.astype(jnp.bfloat16), w_qkv[layer_index]) + b_qkv[layer_index]
        qkv_low = qkv_all.astype(jnp.bfloat16).reshape(seqs_here, tok_here, 3 * model_width)
        queries = split_heads(qkv_low[:, :, :model_width])
        window = extended(qkv_low[:, :, model_width:], (("wide", 1),), rim_rows)
        key_all = with_prefix(layer_index, 0, window[:, :, :model_width])
        value_all = with_prefix(layer_index, 1, window[:, :, model_width:])
        scores = score_block(queries, key_all)
        top_score = jnp.max(scores, axis=2, keepdims=True)
        exp_scores = jnp.exp(scores - top_score)
        denominator = jnp.sum(exp_scores, axis=2, keepdims=True)
        probs_low = (exp_scores / denominator).astype(jnp.bfloat16)
        log_total = top_score + jnp.log(denominator)
        context = jnp.einsum(
            "shkq,skhe->sqhe", probs_low, value_all, preferred_element_type=jnp.float32
        )
        context_low = context.astype(jnp.bfloat16).reshape(rows_here, model_width)
        attention = multiply(context_low, w_out[layer_index]) + b_out[layer_index]
        pre_norm = hidden + attention
        normed = normalize(pre_norm, norm_gain[layer_index, 0], norm_bias[layer_index, 0])
        normed_low = normed.astype(jnp.bfloat16)
        up_rows = lax.all_gather(w_up[layer_index], "wide", axis=0, tiled=True)
        down_rows = lax.all_gather(w_down[layer_index], "wide", axis=0, tiled=True)
        bias_rows = lax.all_gather(b_up[layer_index], "wide", axis=0, tiled=True)
        pre_rows = multiply_back(normed_low, up_rows) + bias_rows.astype(jnp.float32)
        ffn_out = multiply(gelu_exact(pre_rows).astype(jnp.bfloat16), down_rows)
        kept_ffn = ()
        second_in = normed + ffn_out + b_down[layer_index]
        stored.append(
            (queries, key_all, value_all, log_total, pre_norm, normed_low, second_in, kept_ffn)
        )
        hidden = normalize(second_in, norm_gain[layer_index, 1], norm_bias[layer_index, 1])
    output = hidden.astype(jnp.bfloat16).reshape(seqs_here, tok_here, model_width)
    grad_hidden = cotangent.astype(jnp.float32).reshape(rows_here, model_width)
    prefix_grads = [None] * LAYERS
    for layer_index in reversed(range(LAYERS)):
        queries, key_all, value_all, log_total, pre_norm, normed_low, second_in, kept_ffn = stored[
            layer_index
        ]
        grad_sum2 = norm_grad(
            second_in, norm_gain[layer_index, 1], norm_bias[layer_index, 1], grad_hidden
        )
        grad_ffn_low = grad_sum2.astype(jnp.bfloat16)
        back_up_rows = lax.all_gather(w_up[layer_index], "wide", axis=0, tiled=True)
        back_down_rows = lax.all_gather(w_down[layer_index], "wide", axis=0, tiled=True)
        back_bias_rows = lax.all_gather(b_up[layer_index], "wide", axis=0, tiled=True)
        back_pre_rows = multiply_back(normed_low, back_up_rows) + back_bias_rows.astype(jnp.float32)
        grad_rows = gelu_back(back_pre_rows, multiply_back(grad_ffn_low, back_down_rows)).astype(
            jnp.bfloat16
        )
        grad_from_ffn = multiply(grad_rows, back_up_rows)
        grad_normed = grad_sum2 + grad_from_ffn
        grad_sum1 = norm_grad(
            pre_norm, norm_gain[layer_index, 0], norm_bias[layer_index, 0], grad_normed
        )
        grad_attn_low = grad_sum1.astype(jnp.bfloat16)
        grad_context = multiply_back(grad_attn_low, w_out[layer_index]).astype(jnp.bfloat16)
        grad_context = split_heads(grad_context.reshape(seqs_here, tok_here, model_width))
        scores = score_block(queries, key_all)
        probs = jnp.exp(scores - log_total)
        probs_low = probs.astype(jnp.bfloat16)
        grad_probs = jnp.einsum(
            "sqhe,skhe->shkq", grad_context, value_all, preferred_element_type=jnp.float32
        )
        row_dot = jnp.sum(probs * grad_probs, axis=2, keepdims=True)
        grad_scores = (probs * (grad_probs - row_dot)).astype(jnp.bfloat16)
        grad_queries = (
            jnp.einsum("shkq,skhe->sqhe", grad_scores, key_all, preferred_element_type=jnp.float32)
            * score_scale
        )
        grad_keys = (
            jnp.einsum("shkq,sqhe->skhe", grad_scores, queries, preferred_element_type=jnp.float32)
            * score_scale
        )
        grad_values = jnp.einsum(
            "shkq,sqhe->skhe", probs_low, grad_context, preferred_element_type=jnp.float32
        )
        key_count = grad_keys.shape[1]
        grad_keys = grad_keys.reshape(seqs_here, key_count, model_width)
        grad_values = grad_values.reshape(seqs_here, key_count, model_width)
        prefix_grads[layer_index] = jnp.stack(
            [
                jnp.sum(grad_keys[:, :prefix_len], axis=0),
                jnp.sum(grad_values[:, :prefix_len], axis=0),
            ],
            axis=0,
        )
        grad_window = jnp.concatenate(
            [grad_keys[:, prefix_len:], grad_values[:, prefix_len:]], axis=2
        )
        grad_kv = grad_window[:, rim_rows : rim_rows + tok_here]
        rim_grads = jnp.concatenate(
            [grad_window[:, :rim_rows], grad_window[:, rim_rows + tok_here :]], axis=1
        )
        returned = extended(rim_grads.astype(jnp.bfloat16), (("wide", 1),), rim_rows).astype(
            rim_grads.dtype
        )
        grad_kv = grad_kv + returned[:, :rim_rows]
        grad_kv = grad_kv + returned[:, 3 * rim_rows :]
        grad_qkv = jnp.concatenate(
            [grad_queries.reshape(seqs_here, tok_here, model_width), grad_kv], axis=2
        )
        grad_qkv = grad_qkv.astype(jnp.bfloat16).reshape(rows_here, 3 * model_width)
        grad_hidden = grad_sum1 + multiply_back(grad_qkv, w_qkv[layer_index])
    grad_prefix = lax.psum(jnp.stack(prefix_grads, axis=0), ("rows", "wide"))
    return (output, grad_hidden.reshape(seqs_here, tok_here, model_width), grad_prefix)


def solution(mesh):
    return jax.shard_map(
        local,
        mesh=mesh,
        in_specs=(
            P("rows", "wide", None),
            P("rows", None),
            P(),
            P(),
            P(),
            P(),
            P(),
            P(),
            P(None, "wide", None),
            P(None, "wide"),
            P(None, "wide", None),
            P(),
            P(),
            P("rows", "wide", None),
        ),
        out_specs=(P("rows", "wide", None), P("rows", "wide", None), P()),
        check_vma=False,
    )
```

profile of v0, /device:TPU:0, one launch (start us, length us, event | category | flops | bytes accessed | tf_op | source)
XLA Modules:
  0.0 841.0 jit_solution(1946470250862313874)
XLA Ops:
  7.2 3.2 fusion.185
  12.1 6.5 add_convert_fusion.3
  21.5 4.4 collective-permute-start
  25.9 2.3 slice.241
  28.2 91.8 %all-gather.1 = bf16[1,4096]{1,0:T(2,128)(2,1)S(1)} all-gather(bf16[1,512]{1,0:T(2,128)(2,1)S(1)} %get-tuple-element.50), channel_id=3, replica_groups=mesh['rows'=4,'wide'=8] {'wide'}, dimensions={1}, use_global_device_ids=true | all-gather | bytes 9216 | tf_op jit(solution)/shard_map/all_gather | solution.py:126
  126.4 3.4 pad_maximum_fusion.2
  130.9 3.4 pad_maximum_fusion.4
  134.3 6.1 copy.49
  140.4 6.7 copy.50
  147.1 10.5 %fusion.193 = (f32[4,16,128]{2,1,0:T(8,128)S(1)}, f32[4,16,448,128]{3,2,1,0:T(8,128)}) fusion(bf16[4,448,16,64]{1,3,2,0:T(8,128)(2,1)} %bitcast.215, bf16[4,128,16,64]{1,3,2,0:T(8,128)(2,1)S(1)} %bitcast.223, pred[4,448,128]{2,1,0:T(8,128)(4,1)S(1)} %concatenate.59), kind=kOutput, calls=%fused_computation.264 | convolution fusion | flops 480763904 | bytes 19660800 | tf_op jit(solution)/shard_map/sqhe,skhe->shkq/dot_general | solution.py:96
  157.6 9.0 %fusion = f32[4,16,128]{2,1,0:T(8,128)S(1)} fusion(f32[4,16,448,128]{3,2,1,0:T(8,128)} %get-tuple-element.52, f32[4,16,128]{2,1,0:T(8,128)S(1)} %get-tuple-element.51), kind=kLoop, calls=%fused_computation.18 | loop fusion | flops 7331840 | bytes 14745600 | tf_op jit(solution)/shard_map/reduce_sum | solution.py:113
  166.7 8.5 %fusion.134 = bf16[4,128,16,64]{1,3,2,0:T(8,128)(2,1)S(1)} fusion(bf16[4,448,16,64]{1,3,2,0:T(8,128)(2,1)S(1)} %bitcast.227, f32[4,16,448,128]{3,2,1,0:T(8,128)} %get-tuple-element.52, f32[4,16,128]{2,1,0:T(8,128)S(1)} %fusion, f32[4,16,128]{2,1,0:T(8,128)S(1)} %get-tuple-element.51), kind=kOutput, calls=%fused_computation.183 | convolution fusion | flops 481296384 | bytes 19464192 | tf_op jit(solution)/shard_map/shkq,skhe->sqhe/dot_general | solution.py:116
  178.0 27.0 %fusion.6 = (f32[512,4096]{1,0:T(8,128)}, f32[512,4096]{1,0:T(8,128)}) fusion(f32[4096]{0:T(1024)S(1)} %bitcast.247, bf16[1,4096,1024]{2,1,0:T(8,128)(2,1)} %all-gather.11.cloned.1.call-done, f32[512,1024]{1,0:T(8,128)S(1)} %get-tuple-element.54, f32[1024]{0:T(1024)} %bitcast.272, f32[1024]{0:T(1024)S(1)} %bitcast.259, f32[512]{0:T(512)S(1)} %fusion.163, ...), kind=kOutput, calls=%fused_computation.26 | convolution fusion | flops 4429709312 | bytes 27291648 | tf_op jit(solution)/shard_map/dot_general | solution.py:48
  205.0 12.3 %fusion.195 = (f32[512]{0:T(512)S(1)}, f32[512,1024]{1,0:T(8,128)S(1)}) fusion(f32[1024]{0:T(1024)S(1)} %bitcast.257, bf16[1,4096,1024]{2,1,0:T(8,128)(2,1)} %all-gather.13.cloned.1.call-done, f32[512,4096]{1,0:T(8,128)} %get-tuple-element.55, f32[512,4096]{1,0:T(8,128)} %get-tuple-element.56, f32[4096]{0:T(1024)S(1)} %bitcast.248, ...), kind=kOutput, calls=%fused_computation.266 | convolution fusion | flops 4307025408 | bytes 29394944 | tf_op jit(solution)/shard_map/dot_general | solution.py:44
  217.7 7.1 add_convert_fusion.2
  227.7 4.4 collective-permute-start.2
  232.2 74.9 %all-gather.4 = bf16[1,4096]{1,0:T(2,128)(2,1)S(1)} all-gather(bf16[1,512]{1,0:T(2,128)(2,1)S(1)} %get-tuple-element.49), channel_id=6, replica_groups=mesh['rows'=4,'wide'=8] {'wide'}, dimensions={1}, use_global_device_ids=true | all-gather | bytes 9216 | tf_op jit(solution)/shard_map/all_gather | solution.py:126
  311.0 3.8 pad_maximum_fusion.3
  314.8 2.5 fusion.183
  319.5 6.1 copy.54
  325.7 4.1 pad_maximum_fusion.6
  329.9 6.3 copy.53
  336.2 10.6 %fusion.196 = (f32[4,16,128]{2,1,0:T(8,128)S(1)}, f32[4,16,448,128]{3,2,1,0:T(8,128)}) fusion(bf16[4,448,16,64]{1,3,2,0:T(8,128)(2,1)} %bitcast.217, bf16[4,128,16,64]{1,3,2,0:T(8,128)(2,1)S(1)} %bitcast.225, pred[4,448,128]{2,1,0:T(8,128)(4,1)S(1)} %concatenate.59), kind=kOutput, calls=%fused_computation.267 | convolution fusion | flops 480763904 | bytes 19660800 | tf_op jit(solution)/shard_map/sqhe,skhe->shkq/dot_general | solution.py:96
  346.8 9.1 %fusion.1 = f32[4,16,128]{2,1,0:T(8,128)S(1)} fusion(f32[4,16,448,128]{3,2,1,0:T(8,128)} %get-tuple-element.60, f32[4,16,128]{2,1,0:T(8,128)S(1)} %get-tuple-element.59), kind=kLoop, calls=%fused_computation.19 | loop fusion | flops 7331840 | bytes 14745600 | tf_op jit(solution)/shard_map/reduce_sum | solution.py:113
  355.9 8.6 %fusion.135 = bf16[4,128,16,64]{1,3,2,0:T(8,128)(2,1)S(1)} fusion(bf16[4,448,16,64]{1,3,2,0:T(8,128)(2,1)S(1)} %bitcast.229, f32[4,16,448,128]{3,2,1,0:T(8,128)} %get-tuple-element.60, f32[4,16,128]{2,1,0:T(8,128)S(1)} %fusion.1, f32[4,16,128]{2,1,0:T(8,128)S(1)} %get-tuple-element.59), kind=kOutput, calls=%fused_computation.184 | convolution fusion | flops 481296384 | bytes 19464192 | tf_op jit(solution)/shard_map/shkq,skhe->sqhe/dot_general | solution.py:116
  367.9 26.7 %fusion.7 = (f32[512,4096]{1,0:T(8,128)}, f32[512,4096]{1,0:T(8,128)}) fusion(f32[4096]{0:T(1024)S(1)} %bitcast.250, bf16[1,4096,1024]{2,1,0:T(8,128)(2,1)} %all-gather.15.cloned.1.call-done, f32[512,1024]{1,0:T(8,128)S(1)} %get-tuple-element.62, f32[1024]{0:T(1024)S(1)} %bitcast.268, f32[1024]{0:T(1024)S(1)} %bitcast.265, f32[512]{0:T(512)S(1)} %fusion.165, ...), kind=kOutput, calls=%fused_computation.27 | convolution fusion | flops 4429709312 | bytes 27291648 | tf_op jit(solution)/shard_map/dot_general | solution.py:48
  394.6 11.0 %fusion.198 = (f32[512]{0:T(512)S(1)}, f32[512,1024]{1,0:T(8,128)S(1)}) fusion(f32[1024]{0:T(1024)S(1)} %bitcast.255, bf16[1,4096,1024]{2,1,0:T(8,128)(2,1)} %all-gather.17.cloned.1.call-done, f32[512,4096]{1,0:T(8,128)} %get-tuple-element.63, f32[512,4096]{1,0:T(8,128)} %get-tuple-element.64, f32[4096]{0:T(1024)S(1)} %bitcast.251, ...), kind=kOutput, calls=%fused_computation.269 | convolution fusion | flops 4307025408 | bytes 29394944 | tf_op jit(solution)/shard_map/dot_general | solution.py:44
  406.2 2.6 fusion.180
  408.8 23.4 %multiply_reduce_fusion.4 = (f32[512]{0:T(512)S(1)}, f32[512,1024]{1,0:T(8,128)}) fusion(f32[512,1024]{1,0:T(8,128)S(1)} %get-tuple-element.62, f32[512]{0:T(512)S(1)} %broadcast_multiply_fusion.3, f32[1024]{0:T(1024)S(1)} %bitcast.267, bf16[1,4096,1024]{2,1,0:T(8,128)(2,1)} %all-gather.15.cloned.1.call-done, f32[512,4096]{1,0:T(8,128)} %get-tuple-element.63, ...), kind=kOutput, calls=%fused_computation.153 | convolution fusion | flops 8625586176 | bytes 39872512 | tf_op jit(solution)/shard_map/dot_general | solution.py:44
  432.3 2.3 fusion.179
  440.4 12.0 %fusion.36 = f32[4,16,64,448]{3,2,1,0:T(8,128)} fusion(bf16[4,128,16,64]{1,3,2,0:T(8,128)(2,1)S(1)} %copy.58, f32[4,16,448,128]{3,2,1,0:T(8,128)} %get-tuple-element.60, f32[4,16,128]{2,1,0:T(8,128)S(1)} %log_add_fusion.1), kind=kOutput, calls=%fused_computation.75 | convolution fusion | flops 477102080 | bytes 23101440 | tf_op jit(solution)/shard_map/shkq,sqhe->skhe/dot_general | solution.py:177
  452.4 10.4 %multiply_reduce_fusion.1 = (f32[4,16,128]{2,1,0:T(8,128)S(1)}, f32[4,16,448,128]{3,2,1,0:T(8,128)}) fusion(f32[4,16,448,128]{3,2,1,0:T(8,128)} %get-tuple-element.60, f32[4,16,128]{2,1,0:T(8,128)S(1)} %log_add_fusion.1, bf16[4,448,16,64]{1,3,2,0:T(8,128)(2,1)S(1)} %bitcast.230, bf16[4,128,16,64]{1,3,2,0:T(8,128)(2,1)S(1)} %copy.58), kind=kOutput, calls=%fused_computation.10 | convolution fusion | flops 480763904 | bytes 34144256 | tf_op jit(solution)/shard_map/sqhe,skhe->shkq/dot_general | solution.py:164
  462.8 7.9 slice.247
  470.6 6.6 copy.81
  477.2 10.5 %multiply_convert_fusion.1 = bf16[4,16,448,128]{3,2,1,0:T(8,128)(2,1)S(1)} fusion(f32[4,16,448,128]{3,2,1,0:T(8,128)} %get-tuple-element.70, f32[4,16,448,128]{3,2,1,0:T(8,128)} %get-tuple-element.60, f32[4,16,128]{2,1,0:T(8,128)S(1)} %get-tuple-element.69, f32[4,16,128]{2,1,0:T(8,128)S(1)} %log_add_fusion.1), kind=kLoop, calls=%fused_computation.9 | loop fusion | flops 14680064 | bytes 36765696 | tf_op jit(solution)/shard_map/convert_element_type | solution.py:168
  487.7 3.2 broadcast_multiply_fusion.1
  491.0 3.3 copy-done.2
  494.3 4.3 slice.246
  498.6 6.6 copy.80
  505.2 8.2 fusion.3
  513.4 4.9 fusion.182
  518.4 3.5 collective-permute-start.4
  523.2 4.8 fusion.136
  531.6 4.1 fusion.61
  536.3 6.6 multiply_reduce_fusion.3
  544.9 23.6 %multiply_reduce_fusion.2 = (f32[512]{0:T(512)S(1)}, f32[512,1024]{1,0:T(8,128)}) fusion(f32[512,1024]{1,0:T(8,128)S(1)} %copy-done.14, f32[512]{0:T(512)S(1)} %copy-done.35, f32[1024]{0:T(1024)S(1)} %bitcast.261, bf16[1,4096,1024]{2,1,0:T(8,128)(2,1)} %all-gather.11.cloned.1.call-done, f32[512,4096]{1,0:T(8,128)} %get-tuple-element.55, ...), kind=kOutput, calls=%fused_computation.148 | convolution fusion | flops 8625586176 | bytes 39872512 | tf_op jit(solution)/shard_map/dot_general | solution.py:44
  568.5 2.3 fusion.177
  576.6 11.8 %fusion.34 = f32[4,16,64,448]{3,2,1,0:T(8,128)} fusion(bf16[4,128,16,64]{1,3,2,0:T(8,128)(2,1)S(1)} %copy.65, f32[4,16,448,128]{3,2,1,0:T(8,128)} %get-tuple-element.52, f32[4,16,128]{2,1,0:T(8,128)S(1)} %log_add_fusion), kind=kOutput, calls=%fused_computation.74 | convolution fusion | flops 477102080 | bytes 23101440 | tf_op jit(solution)/shard_map/shkq,sqhe->skhe/dot_general | solution.py:177
  588.5 10.1 %multiply_reduce_fusion = (f32[4,16,128]{2,1,0:T(8,128)S(1)}, f32[4,16,448,128]{3,2,1,0:T(8,128)}) fusion(f32[4,16,448,128]{3,2,1,0:T(8,128)} %get-tuple-element.52, f32[4,16,128]{2,1,0:T(8,128)S(1)} %log_add_fusion, bf16[4,448,16,64]{1,3,2,0:T(8,128)(2,1)S(1)} %bitcast.228, bf16[4,128,16,64]{1,3,2,0:T(8,128)(2,1)S(1)} %copy.65), kind=kOutput, calls=%fused_computation.7 | convolution fusion | flops 480763904 | bytes 34144256 | tf_op jit(solution)/shard_map/sqhe,skhe->shkq/dot_general | solution.py:164
  598.6 7.7 slice.253
  606.3 6.6 copy.83
  612.9 10.7 %multiply_convert_fusion = bf16[4,16,448,128]{3,2,1,0:T(8,128)(2,1)S(1)} fusion(f32[4,16,448,128]{3,2,1,0:T(8,128)} %get-tuple-element.76, f32[4,16,448,128]{3,2,1,0:T(8,128)} %get-tuple-element.52, f32[4,16,128]{2,1,0:T(8,128)S(1)} %get-tuple-element.75, f32[4,16,128]{2,1,0:T(8,128)S(1)} %log_add_fusion), kind=kLoop, calls=%fused_computation.6 | loop fusion | flops 14680064 | bytes 36765696 | tf_op jit(solution)/shard_map/convert_element_type | solution.py:168
  623.6 3.2 broadcast_multiply_fusion
  626.9 3.3 copy-done.3
  630.1 4.3 slice.252
  634.4 6.6 copy.82
  641.0 8.2 fusion.2
  649.3 4.9 fusion.181
  654.1 19.9 %collective-permute-start.6 = (bf16[4,128,2048]{2,1,0:T(8,128)(2,1)}, bf16[4,128,2048]{2,1,0:T(8,128)(2,1)}, u32[]{:S(2)}, u32[]{:S(2)}) collective-permute-start(bf16[4,128,2048]{2,1,0:T(8,128)(2,1)} %get-tuple-element.16), channel_id=1, source_target_pairs={{0,1},{1,2},{2,3},{3,4},{4,5},{5,6},{6,7},{8,9},{9,10},{10,11},{11... | collective-permute-start | bytes 6291464 | tf_op jit(solution)/shard_map/ppermute | solution.py:17
  684.1 6.0 fusion.137
  693.5 125.9 %all-reduce.4.cloned.1.call-done = f32[2,2,64,1024]{2,3,1,0:T(8,128)} async-done(((f32[2,2,64,1024]{2,3,1,0:T(8,128)}), f32[2,2,64,1024]{2,3,1,0:T(8,128)}) %all-reduce.4.cloned.1.call-update) | async-done | bytes 1048592 | tf_op jit(solution)/shard_map/psum | solution.py:207
  819.4 3.1 copy.71
  822.6 4.0 fusion.57
  826.6 7.5 add_add_fusion.8
  (232 shorter events, 60.6 us)
Async XLA Ops:
  7.2 4.9 copy-start.32
  7.2 4.9 copy-start.68
  7.2 170.8 %all-gather.11.cloned.1.call-start = ((), (), s32[]{:S(2)}) async-start(), calls=%async_computation.1 | async-start | bytes 9437184 | tf_op jit(solution)/shard_map/all_gather | solution.py:124
  10.4 194.5 %all-gather.13.cloned.1.call-start = ((), (), s32[]{:S(2)}) async-start(), calls=%async_computation.2 | async-start | bytes 9437184 | tf_op jit(solution)/shard_map/all_gather | solution.py:125
  12.0 355.8 %all-gather.15.cloned.1.call-start = ((), (), s32[]{:S(2)}) async-start(), calls=%async_computation.3 | async-start | bytes 9437184 | tf_op jit(solution)/shard_map/all_gather | solution.py:124
  18.6 9.6 %copy-start.53 = (bf16[2,512]{1,0:T(2,128)(2,1)S(1)}, bf16[2,512]{1,0:T(2,128)(2,1)}, u32[]{:S(2)}) copy-start(bf16[2,512]{1,0:T(2,128)(2,1)} %param.23) | copy-start | bytes 6148
  18.6 103.1 %copy-start.33 = (s32[4,1024]{1,0:T(4,128)S(1)}, s32[4,1024]{1,0:T(4,128)}, u32[]{:S(2)}) copy-start(s32[4,1024]{1,0:T(4,128)} %param.15) | copy-start | bytes 49156
  18.6 103.4 %copy-start.51 = (f32[2,1024]{1,0:T(2,128)S(1)}, f32[2,1024]{1,0:T(2,128)}, u32[]{:S(2)}) copy-start(f32[2,1024]{1,0:T(2,128)} %param.19) | copy-start | bytes 24580
  18.6 104.0 %copy-start.52 = (f32[2,1024]{1,0:T(2,128)S(1)}, f32[2,1024]{1,0:T(2,128)}, u32[]{:S(2)}) copy-start(f32[2,1024]{1,0:T(2,128)} %param.25) | copy-start | bytes 24580
  18.6 104.6 %copy-start.43 = (f32[2,2,1024]{2,1,0:T(2,128)S(1)}, f32[2,2,1024]{2,1,0:T(2,128)}, u32[]{:S(2)}) copy-start(f32[2,2,1024]{2,1,0:T(2,128)} %param.20) | copy-start | bytes 49156
  18.6 105.2 %copy-start.44 = (f32[2,2,1024]{2,1,0:T(2,128)S(1)}, f32[2,2,1024]{2,1,0:T(2,128)}, u32[]{:S(2)}) copy-start(f32[2,2,1024]{2,1,0:T(2,128)} %param.21) | copy-start | bytes 49156
  20.2 106.2 %collective-permute-start.1 = (bf16[4,128,2048]{2,1,0:T(8,128)(2,1)S(1)}, bf16[4,128,2048]{2,1,0:T(8,128)(2,1)}, u32[]{:S(2)}, u32[]{:S(2)}) collective-permute-start(bf16[4,128,2048]{2,1,0:T(8,128)(2,1)S(1)} %slice.238), channel_id=1, source_target_pairs={{1,0},{2,1},{3,2},{4,3},{5,4},{6,5},{7,6},{9,8},{10,9},{11,10},{12... | collective-permute-start | bytes 6291464 | tf_op jit(solution)/shard_map/ppermute | solution.py:20
  21.5 104.9 %collective-permute-start = (bf16[4,128,2048]{2,1,0:T(8,128)(2,1)S(1)}, bf16[4,128,2048]{2,1,0:T(8,128)(2,1)}, u32[]{:S(2)}, u32[]{:S(2)}) collective-permute-start(bf16[4,128,2048]{2,1,0:T(8,128)(2,1)S(1)} %slice.238), channel_id=1, source_target_pairs={{0,1},{1,2},{2,3},{3,4},{4,5},{5,6},{6,7},{8,9},{9,10},{10,11},{11... | collective-permute-start | bytes 6291464 | tf_op jit(solution)/shard_map/ppermute | solution.py:17
  25.9 368.6 %all-gather.17.cloned.1.call-start = ((), (), s32[]{:S(2)}) async-start(), calls=%async_computation.4 | async-start | bytes 9437184 | tf_op jit(solution)/shard_map/all_gather | solution.py:125
  120.0 84.9 %copy-start.45 = (f32[1,4096]{1,0:T(1,128)}, f32[1,4096]{1,0:T(1,128)S(1)}, u32[]{:S(2)}) copy-start(f32[1,4096]{1,0:T(1,128)S(1)} %convert_element_type.132) | copy-start | bytes 49156
  121.7 25.4 %copy-start.5 = (bf16[4,128,1024]{1,2,0:T(8,128)(2,1)}, bf16[4,128,1024]{1,2,0:T(8,128)(2,1)S(1)}, u32[]{:S(2)}) copy-start(bf16[4,128,1024]{1,2,0:T(8,128)(2,1)S(1)} %copy.51) | copy-start | bytes 3145732
  123.8 81.1 %copy-start.56 = (f32[1,1,1024]{2,1,0:T(1,128)}, f32[1,1,1024]{2,1,0:T(1,128)S(1)}, u32[]{:S(2)}) copy-start(f32[1,1,1024]{2,1,0:T(1,128)S(1)} %get-tuple-element.37) | copy-start | bytes 12292
  123.8 241.5 %copy-start.58 = (f32[1,1,1024]{2,1,0:T(1,128)}, f32[1,1,1024]{2,1,0:T(1,128)S(1)}, u32[]{:S(2)}) copy-start(f32[1,1,1024]{2,1,0:T(1,128)S(1)} %get-tuple-element.36) | copy-start | bytes 12292
  157.6 9.1 %copy-start.27 = (f32[4,16,128]{2,1,0:T(8,128)}, f32[4,16,128]{2,1,0:T(8,128)S(1)}, u32[]{:S(2)}) copy-start(f32[4,16,128]{2,1,0:T(8,128)S(1)} %get-tuple-element.51) | copy-start | bytes 98308
  157.6 9.1 %copy-start.9 = (bf16[4,448,1024]{1,2,0:T(8,128)(2,1)S(1)}, bf16[4,448,1024]{1,2,0:T(8,128)(2,1)}, u32[]{:S(2)}) copy-start(bf16[4,448,1024]{1,2,0:T(8,128)(2,1)} %copy.49) | copy-start | bytes 11010052
  166.6 8.6 %copy-start.29 = (f32[4,16,128]{2,1,0:T(8,128)}, f32[4,16,128]{2,1,0:T(8,128)S(1)}, u32[]{:S(2)}) copy-start(f32[4,16,128]{2,1,0:T(8,128)S(1)} %fusion) | copy-start | bytes 98308
  166.7 9.4 %copy-start.64 = (bf16[2,1024,1024]{2,1,0:T(8,128)(2,1)S(1)}, bf16[2,1024,1024]{2,1,0:T(8,128)(2,1)}, u32[]{:S(2)}) copy-start(bf16[2,1024,1024]{2,1,0:T(8,128)(2,1)} %param.18) | copy-start | bytes 12582916
  166.7 9.4 %copy-start.69 = (bf16[4,128,1024]{2,1,0:T(8,128)(2,1)S(1)}, bf16[4,128,1024]{2,1,0:T(8,128)(2,1)}, u32[]{:S(2)}) copy-start(bf16[4,128,1024]{2,1,0:T(8,128)(2,1)} %param.14) | copy-start | bytes 3145732
  177.5 27.4 %copy-start.13 = (f32[512,1024]{1,0:T(8,128)}, f32[512,1024]{1,0:T(8,128)S(1)}, u32[]{:S(2)}) copy-start(f32[512,1024]{1,0:T(8,128)S(1)} %get-tuple-element.54) | copy-start | bytes 6291460
  177.6 27.4 %copy-start.34 = (f32[512]{0:T(512)}, f32[512]{0:T(512)S(1)}, u32[]{:S(2)}) copy-start(f32[512]{0:T(512)S(1)} %broadcast_multiply_fusion.5) | copy-start | bytes 6148
  177.9 27.0 %copy-start.38 = (f32[512]{0:T(512)}, f32[512]{0:T(512)S(1)}, u32[]{:S(2)}) copy-start(f32[512]{0:T(512)S(1)} %multiply_reduce_fusion.8) | copy-start | bytes 6148
  177.9 27.1 %copy-start.47 = (f32[512]{0:T(512)}, f32[512]{0:T(512)S(1)}, u32[]{:S(2)}) copy-start(f32[512]{0:T(512)S(1)} %fusion.163) | copy-start | bytes 6148
  178.0 27.0 %copy-start.63 = (f32[1,1,1024]{2,1,0:T(1,128)S(1)}, f32[1,1,1024]{2,1,0:T(1,128)}, u32[]{:S(2)}) copy-start(f32[1,1,1024]{2,1,0:T(1,128)} %get-tuple-element.41) | copy-start | bytes 12292
  205.0 12.7 %copy-start.62 = (f32[1,1,1024]{2,1,0:T(1,128)S(1)}, f32[1,1,1024]{2,1,0:T(1,128)}, u32[]{:S(2)}) copy-start(f32[1,1,1024]{2,1,0:T(1,128)} %get-tuple-element.40) | copy-start | bytes 12292
  217.3 7.5 copy-start.15
  217.3 148.0 %copy-start.36 = (f32[512]{0:T(512)}, f32[512]{0:T(512)S(1)}, u32[]{:S(2)}) copy-start(f32[512]{0:T(512)S(1)} %broadcast_multiply_fusion.4) | copy-start | bytes 6148
  217.7 7.1 copy-start.40
  217.7 147.6 %copy-start.49 = (f32[512]{0:T(512)}, f32[512]{0:T(512)S(1)}, u32[]{:S(2)}) copy-start(f32[512]{0:T(512)S(1)} %fusion.164) | copy-start | bytes 6148
  226.4 84.6 %collective-permute-start.3 = (bf16[4,128,2048]{2,1,0:T(8,128)(2,1)S(1)}, bf16[4,128,2048]{2,1,0:T(8,128)(2,1)}, u32[]{:S(2)}, u32[]{:S(2)}) collective-permute-start(bf16[4,128,2048]{2,1,0:T(8,128)(2,1)S(1)} %slice.242), channel_id=1, source_target_pairs={{1,0},{2,1},{3,2},{4,3},{5,4},{6,5},{7,6},{9,8},{10,9},{11,10},{12... | collective-permute-start | bytes 6291464 | tf_op jit(solution)/shard_map/ppermute | solution.py:20
  227.7 83.3 %collective-permute-start.2 = (bf16[4,128,2048]{2,1,0:T(8,128)(2,1)S(1)}, bf16[4,128,2048]{2,1,0:T(8,128)(2,1)}, u32[]{:S(2)}, u32[]{:S(2)}) collective-permute-start(bf16[4,128,2048]{2,1,0:T(8,128)(2,1)S(1)} %slice.242), channel_id=1, source_target_pairs={{0,1},{1,2},{2,3},{3,4},{4,5},{5,6},{6,7},{8,9},{9,10},{10,11},{11... | collective-permute-start | bytes 6291464 | tf_op jit(solution)/shard_map/ppermute | solution.py:17
  232.1 587.3 %all-reduce.4.cloned.1.call-start = ((), (), s32[]{:S(2)}) async-start(), calls=%async_computation | async-start | bytes 4194304 | tf_op jit(solution)/shard_map/psum | solution.py:207
  311.0 25.2 %copy-start.7 = (bf16[4,128,1024]{1,2,0:T(8,128)(2,1)}, bf16[4,128,1024]{1,2,0:T(8,128)(2,1)S(1)}, u32[]{:S(2)}) copy-start(bf16[4,128,1024]{1,2,0:T(8,128)(2,1)S(1)} %copy.55) | copy-start | bytes 3145732
  346.8 9.1 %copy-start.11 = (bf16[4,448,1024]{1,2,0:T(8,128)(2,1)S(1)}, bf16[4,448,1024]{1,2,0:T(8,128)(2,1)}, u32[]{:S(2)}) copy-start(bf16[4,448,1024]{1,2,0:T(8,128)(2,1)} %copy.53) | copy-start | bytes 11010052
  355.8 9.5 %copy-start.16 = (f32[512,1024]{1,0:T(8,128)S(1)}, f32[512,1024]{1,0:T(8,128)}, u32[]{:S(2)}) copy-start(f32[512,1024]{1,0:T(8,128)} %copy-done.15) | copy-start | bytes 6291460
  355.8 9.5 %copy-start.55 = (f32[1,1024]{1,0:T(1,128)S(1)}, f32[1,1024]{1,0:T(1,128)}, u32[]{:S(2)}) copy-start(f32[1,1024]{1,0:T(1,128)} %get-tuple-element.45) | copy-start | bytes 12292
  355.8 9.5 %copy-start.65 = (bf16[2,1024,1024]{2,1,0:T(8,128)(2,1)S(1)}, bf16[2,1024,1024]{2,1,0:T(8,128)(2,1)}, u32[]{:S(2)}) copy-start(bf16[2,1024,1024]{2,1,0:T(8,128)(2,1)} %param.18) | copy-start | bytes 12582916
  367.9 26.7 %copy-start.54 = (f32[1,1024]{1,0:T(1,128)S(1)}, f32[1,1024]{1,0:T(1,128)}, u32[]{:S(2)}) copy-start(f32[1,1024]{1,0:T(1,128)} %get-tuple-element.43) | copy-start | bytes 12292
  394.5 11.0 %copy-start.18 = (bf16[4,128,1024]{2,1,0:T(8,128)(2,1)S(1)}, bf16[4,128,1024]{2,1,0:T(8,128)(2,1)}, u32[]{:S(2)}) copy-start(bf16[4,128,1024]{2,1,0:T(8,128)(2,1)} %param.27) | copy-start | bytes 3145732
  394.5 11.0 %copy-start.31 = (f32[1,1,1024]{2,1,0:T(1,128)S(1)}, f32[1,1,1024]{2,1,0:T(1,128)}, u32[]{:S(2)}) copy-start(f32[1,1,1024]{2,1,0:T(1,128)} %get-tuple-element.35) | copy-start | bytes 12292
  394.5 11.7 %copy-start.42 = (f32[1,1,1024]{2,1,0:T(1,128)S(1)}, f32[1,1,1024]{2,1,0:T(1,128)}, u32[]{:S(2)}) copy-start(f32[1,1,1024]{2,1,0:T(1,128)} %get-tuple-element.39) | copy-start | bytes 12292
  440.4 12.0 %copy-start.12 = (bf16[4,448,1024]{1,2,0:T(8,128)(2,1)S(1)}, bf16[4,448,1024]{1,2,0:T(8,128)(2,1)}, u32[]{:S(2)}) copy-start(bf16[4,448,1024]{1,2,0:T(8,128)(2,1)} %copy.53) | copy-start | bytes 11010052
  477.2 10.5 %copy-start.8 = (bf16[4,128,1024]{1,2,0:T(8,128)(2,1)S(1)}, bf16[4,128,1024]{1,2,0:T(8,128)(2,1)}, u32[]{:S(2)}) copy-start(bf16[4,128,1024]{1,2,0:T(8,128)(2,1)} %copy-done.7) | copy-start | bytes 3145732
  513.4 9.7 %copy-start.28 = (f32[4,16,128]{2,1,0:T(8,128)S(1)}, f32[4,16,128]{2,1,0:T(8,128)}, u32[]{:S(2)}) copy-start(f32[4,16,128]{2,1,0:T(8,128)} %copy-done.27) | copy-start | bytes 98308
  513.4 9.7 %copy-start.30 = (f32[4,16,128]{2,1,0:T(8,128)S(1)}, f32[4,16,128]{2,1,0:T(8,128)}, u32[]{:S(2)}) copy-start(f32[4,16,128]{2,1,0:T(8,128)} %copy-done.29) | copy-start | bytes 98308
  513.4 9.7 %copy-start.4 = (bf16[4,448,1024]{1,2,0:T(8,128)(2,1)S(1)}, bf16[4,448,1024]{1,2,0:T(8,128)(2,1)}, u32[]{:S(2)}) copy-start(bf16[4,448,1024]{1,2,0:T(8,128)(2,1)} %copy.54) | copy-start | bytes 11010052
  518.4 13.3 %collective-permute-start.4 = (bf16[4,128,2048]{2,1,0:T(8,128)(2,1)}, bf16[4,128,2048]{2,1,0:T(8,128)(2,1)}, u32[]{:S(2)}, u32[]{:S(2)}) collective-permute-start(bf16[4,128,2048]{2,1,0:T(8,128)(2,1)} %get-tuple-element.18), channel_id=1, source_target_pairs={{0,1},{1,2},{2,3},{3,4},{4,5},{5,6},{6,7},{8,9},{9,10},{10,11},{11... | collective-permute-start | bytes 6291464 | tf_op jit(solution)/shard_map/ppermute | solution.py:17
  521.8 9.8 %collective-permute-start.5 = (bf16[4,128,2048]{2,1,0:T(8,128)(2,1)}, bf16[4,128,2048]{2,1,0:T(8,128)(2,1)}, u32[]{:S(2)}, u32[]{:S(2)}) collective-permute-start(bf16[4,128,2048]{2,1,0:T(8,128)(2,1)} %get-tuple-element.19), channel_id=1, source_target_pairs={{1,0},{2,1},{3,2},{4,3},{5,4},{6,5},{7,6},{9,8},{10,9},{11,10},{12... | collective-permute-start | bytes 6291464 | tf_op jit(solution)/shard_map/ppermute | solution.py:20
  531.6 4.1 copy-start.17
  531.6 4.7 copy-start.25
  531.6 4.7 copy-start.37
  531.6 4.7 copy-start.59
  536.3 6.7 copy-start.41
  536.3 6.7 copy-start.50
  544.9 23.7 %copy-start.39 = (f32[512]{0:T(512)S(1)}, f32[512]{0:T(512)}, u32[]{:S(2)}) copy-start(f32[512]{0:T(512)} %copy-done.38) | copy-start | bytes 6148
  544.9 23.7 %copy-start.48 = (f32[512]{0:T(512)S(1)}, f32[512]{0:T(512)}, u32[]{:S(2)}) copy-start(f32[512]{0:T(512)} %copy-done.47) | copy-start | bytes 6148
  576.6 11.8 %copy-start.10 = (bf16[4,448,1024]{1,2,0:T(8,128)(2,1)S(1)}, bf16[4,448,1024]{1,2,0:T(8,128)(2,1)}, u32[]{:S(2)}) copy-start(bf16[4,448,1024]{1,2,0:T(8,128)(2,1)} %copy.49) | copy-start | bytes 11010052
  612.9 10.7 %copy-start.6 = (bf16[4,128,1024]{1,2,0:T(8,128)(2,1)S(1)}, bf16[4,128,1024]{1,2,0:T(8,128)(2,1)}, u32[]{:S(2)}) copy-start(bf16[4,128,1024]{1,2,0:T(8,128)(2,1)} %copy-done.5) | copy-start | bytes 3145732
  654.1 168.4 %collective-permute-start.6 = (bf16[4,128,2048]{2,1,0:T(8,128)(2,1)}, bf16[4,128,2048]{2,1,0:T(8,128)(2,1)}, u32[]{:S(2)}, u32[]{:S(2)}) collective-permute-start(bf16[4,128,2048]{2,1,0:T(8,128)(2,1)} %get-tuple-element.16), channel_id=1, source_target_pairs={{0,1},{1,2},{2,3},{3,4},{4,5},{5,6},{6,7},{8,9},{9,10},{10,11},{11... | collective-permute-start | bytes 6291464 | tf_op jit(solution)/shard_map/ppermute | solution.py:17
  674.0 148.6 %collective-permute-start.7 = (bf16[4,128,2048]{2,1,0:T(8,128)(2,1)}, bf16[4,128,2048]{2,1,0:T(8,128)(2,1)}, u32[]{:S(2)}, u32[]{:S(2)}) collective-permute-start(bf16[4,128,2048]{2,1,0:T(8,128)(2,1)} %get-tuple-element.17), channel_id=1, source_target_pairs={{1,0},{2,1},{3,2},{4,3},{5,4},{6,5},{7,6},{9,8},{10,9},{11,10},{12... | collective-permute-start | bytes 6291464 | tf_op jit(solution)/shard_map/ppermute | solution.py:20
  (19 other events, 48.9 us)
Sparse Core Ops, SparseCore 0:
  10.6 101.7 all-gather.10
  114.6 85.6 all-gather.12
  201.9 97.0 all-gather.14
  301.0 86.1 all-gather.16
  684.2 135.1 all-reduce.3
where the time goes:
time: 847 us; the launch traced here: 841 us
  matrix products  257 us (30%)
  blocking collectives  167 us (20%)
  local copies, waits for them, and re-layouts  137 us (16%)
  waiting for transfers between devices  126 us (15%)
  other arithmetic  101 us (12%)
  starting transfers between devices  37.4 us (4%)
  between operations  15.4 us (2%)
    all_gather x2, blocking collectives, local(): bias_rows = lax.all_gather(b_up[layer_index], 'wide', axis=0, tiled=True)  167 us
    psum x1, waiting for transfers between devices, local(): grad_prefix = lax.psum(jnp.stack(prefix_grads, axis=0), ('rows', 'wide'))  126 us
    dot_general x8, matrix products, multiply(): return jnp.dot(left, right, preferred_element_type=jnp.float32)  86.8 us
    dot_general x6, matrix products, multiply_back(): lax.dot_general(left, right, (((1,), (1,)), ((), ())), preferred_element_...  70.4 us
    unnamed x145, local copies, waits for them, and re-layouts  42.3 us
    ppermute x4, starting transfers between devices, extended(): lax.ppermute(lax.slice_in_dim(block, block.shape[dim] - width, None, axis...  32.1 us
    concatenate x4, local copies, waits for them, and re-layouts, with_prefix(): return split_heads(jnp.concatenate([fixed_rows, window_part], axis=1))  25.2 us
    another operation x4, other arithmetic  24.5 us
  transfers between devices with their start and end apart: 13, of which 1 were waited for; matrix products, arithmetic and copies ran while one was open for 28% of the time, Pallas kernels for 0%

commit v1 on v0

--- a/solution.py
+++ b/solution.py
@@ -123,7 +123,19 @@
         normed_low = normed.astype(jnp.bfloat16)
         up_rows = lax.all_gather(w_up[layer_index], "wide", axis=0, tiled=True)
         down_rows = lax.all_gather(w_down[layer_index], "wide", axis=0, tiled=True)
-        bias_rows = lax.all_gather(b_up[layer_index], "wide", axis=0, tiled=True)
+        ways, here, step = (
+            lax.axis_size("wide"),
+            lax.axis_index("wide"),
+            b_up[layer_index].shape[0],
+        )
+        line, have = (b_up[layer_index], 1)
+        while have < ways:
+            line = jnp.concatenate(
+                [line, lax.ppermute(line, "wide", [(d, (d - have) % ways) for d in range(ways)])],
+                axis=0,
+            )
+            have = 2 * have
+        bias_rows = jnp.roll(line, here * step, axis=0)
         pre_rows = multiply_back(normed_low, up_rows) + bias_rows.astype(jnp.float32)
         ffn_out = multiply(gelu_exact(pre_rows).astype(jnp.bfloat16), down_rows)
         kept_ffn = ()

time: 847 us -> 908 us (1.072)
  blocking collectives: 167 us -> 48.3 us
  starting transfers between devices: 37.4 us -> 153 us
  matrix products: 257 us -> 297 us
  waiting for transfers between devices: 126 us -> 145 us
    ppermute x0 -> x6, starting transfers between devices: none -> 131 us  [local(): lax.ppermute(line, 'wide', [(d, (d - have) % ways) for d in range(ways)])]
    all_gather x2, blocking collectives: 167 us -> 48.3 us  [local(): lax.all_gather(b_up[layer_index], 'wide', axis=0, tiled=True)]
    dot_general x8, matrix products: 86.8 us -> 144 us  [multiply(): return jnp.dot(left, right, preferred_element_type=jnp.float32)]
    ppermute x0 -> x6, waiting for transfers between devices: none -> 18.6 us  [local(): lax.ppermute(line, 'wide', [(d, (d - have) % ways) for d in range(ways)])]
    ppermute x4, starting transfers between devices: 32.1 us -> 16 us  [extended(): lax.ppermute(lax.slice_in_dim(block, block.shape[dim] - width, None, axis...]
    dot_general x6, matrix products: 70.4 us -> 54.4 us  [multiply_back(): lax.dot_general(left, right, (((1,), (1,)), ((), ())), preferred_element_...]
    unnamed x145 -> x157, local copies, waits for them, and re-layouts: 42.3 us -> 43.3 us
  transfers between devices with their start and end apart: 13 -> 19, of which waited for: 1 -> 4; matrix products, arithmetic and copies ran while one was open for 28% -> 25% of each run, Pallas kernels for 0% -> 0%
where the time goes in v1:
time: 908 us; the launch traced here: 902 us
  matrix products  297 us (33%)
  starting transfers between devices  153 us (17%)
  waiting for transfers between devices  145 us (16%)
  local copies, waits for them, and re-layouts  140 us (15%)
  other arithmetic  103 us (11%)
  blocking collectives  48.3 us (5%)
  between operations  15.3 us (2%)
    dot_general x8, matrix products, multiply(): return jnp.dot(left, right, preferred_element_type=jnp.float32)  144 us
    ppermute x6, starting transfers between devices, local(): lax.ppermute(line, 'wide', [(d, (d - have) % ways) for d in range(ways)])  131 us
    psum x1, waiting for transfers between devices, local(): grad_prefix = lax.psum(jnp.stack(prefix_grads, axis=0), ('rows', 'wide'))  125 us
    dot_general x6, matrix products, multiply_back(): lax.dot_general(left, right, (((1,), (1,)), ((), ())), preferred_element_...  54.4 us
    all_gather x2, blocking collectives, local(): lax.all_gather(b_up[layer_index], 'wide', axis=0, tiled=True)  48.3 us
    unnamed x157, local copies, waits for them, and re-layouts  43.3 us
    concatenate x4, local copies, waits for them, and re-layouts, with_prefix(): return split_heads(jnp.concatenate([fixed_rows, window_part], axis=1))  25.4 us
    another operation x4, other arithmetic  24.6 us
  transfers between devices with their start and end apart: 19, of which 4 were waited for; matrix products, arithmetic and copies ran while one was open for 25% of the time, Pallas kernels for 0%

profile of v1, /device:TPU:0, one launch (start us, length us, event | category | flops | bytes accessed | tf_op | source)
XLA Modules:
  0.0 901.8 jit_solution(8300551225836706957)
XLA Ops:
  7.2 3.1 fusion.417
  14.9 6.5 add_convert_fusion.1
  24.4 4.4 collective-permute-start
  29.9 4.0 collective-permute-start.2
  37.1 61.6 %collective-permute-start.3 = (bf16[1024]{0:T(1024)(128)(2,1)S(1)}, bf16[1024]{0:T(1024)(128)(2,1)S(1)}, u32[]{:S(2)}, u32[]{:S(2)}) collective-permute-start(bf16[1024]{0:T(1024)(128)(2,1)S(1)} %pad_maximum_fusion.17), channel_id=1, source_target_pairs={{0,6},{1,7},{2,0},{3,1},{4,2},{5,3},{6,4},{7,5},{8,14},{9,15},{10,... | collective-permute-start | bytes 6152 | tf_op jit(solution)/shard_map/ppermute | solution.py:134
  99.3 15.9 %collective-permute-done.3 = bf16[1024]{0:T(1024)(128)(2,1)S(1)} collective-permute-done((bf16[1024]{0:T(1024)(128)(2,1)S(1)}, bf16[1024]{0:T(1024)(128)(2,1)S(1)}, u32[]{:S(2)}, u32[]{:S(2)}) %collective-permute-start.3) | collective-permute-done | bytes 2080 | tf_op jit(solution)/shard_map/ppermute | solution.py:134
  115.2 3.6 collective-permute-start.4
  124.8 3.6 pad_maximum_fusion.2
  129.6 3.4 pad_maximum_fusion.4
  133.0 6.2 copy.49
  139.2 6.5 copy.50
  145.7 10.5 %fusion.424 = (f32[4,16,128]{2,1,0:T(8,128)S(1)}, f32[4,16,448,128]{3,2,1,0:T(8,128)}) fusion(bf16[4,448,16,64]{1,3,2,0:T(8,128)(2,1)} %bitcast.211, bf16[4,128,16,64]{1,3,2,0:T(8,128)(2,1)S(1)} %bitcast.219, pred[4,448,128]{2,1,0:T(8,128)(4,1)S(1)} %concatenate.84), kind=kOutput, calls=%fused_computation.519 | convolution fusion | flops 480763904 | bytes 19660800 | tf_op jit(solution)/shard_map/sqhe,skhe->shkq/dot_general | solution.py:96
  156.3 9.0 fusion
  165.3 8.6 fusion.236
  177.4 23.9 %fusion.36 = f32[512,4096]{1,0:T(8,128)} fusion(bf16[1,4096,1024]{2,1,0:T(8,128)(2,1)} %all-gather.11.cloned.1.call-done, f32[512,1024]{1,0:T(8,128)S(1)} %get-tuple-element.57, f32[1024]{0:T(1024)S(1)} %bitcast.264, f32[1024]{0:T(1024)S(1)} %bitcast.251, f32[512]{0:T(512)S(1)} %fusion.281, f32[512]{0:T(512)S(1)} %broadcast_multiply_fusion.5), kind=kOutput, calls=%fused_computation.58 | convolution fusion | flops 4297588736 | bytes 18886656 | tf_op jit(solution)/shard_map/dot_general | solution.py:48
  201.3 26.3 %fusion.426 = (f32[512]{0:T(512)S(1)}, f32[512,1024]{1,0:T(8,128)S(1)}) fusion(f32[1024]{0:T(1024)S(1)} %bitcast.249, bf16[1,4096,1024]{2,1,0:T(8,128)(2,1)} %all-gather.13.cloned.1.call-done, f32[512,4096]{1,0:T(8,128)} %fusion.36, f32[4096]{0:T(1024)S(1)} %fusion.277, f32[1024]{0:T(1024)S(1)} %bitcast.265, f32[1024]{0:T(1024)S(1)} %bitcast.252, ...), kind=kOutput, calls=%fused_computation.521 | convolution fusion | flops 4437048832 | bytes 21006336 | tf_op jit(solution)/shard_map/dot_general | solution.py:44
  228.9 6.7 add_convert_fusion
  237.1 4.4 collective-permute-start.5
  242.8 60.0 %collective-permute-start.8 = (bf16[1024]{0:T(1024)(128)(2,1)S(1)}, bf16[1024]{0:T(1024)(128)(2,1)S(1)}, u32[]{:S(2)}, u32[]{:S(2)}) collective-permute-start(bf16[1024]{0:T(1024)(128)(2,1)S(1)} %pad_maximum_fusion.18), channel_id=1, source_target_pairs={{0,6},{1,7},{2,0},{3,1},{4,2},{5,3},{6,4},{7,5},{8,14},{9,15},{10,... | collective-permute-start | bytes 6152 | tf_op jit(solution)/shard_map/ppermute | solution.py:134
  306.1 13.1 %all-gather.4 = bf16[1,4096]{1,0:T(2,128)(2,1)S(1)} all-gather(bf16[1,512]{1,0:T(2,128)(2,1)S(1)} %copy-done.59), channel_id=6, replica_groups=mesh['rows'=4,'wide'=8] {'wide'}, dimensions={1}, use_global_device_ids=true | all-gather | bytes 9216 | tf_op jit(solution)/shard_map/all_gather | solution.py:160
  322.7 3.5 pad_maximum_fusion.3
  331.2 6.1 copy.54
  337.4 4.1 pad_maximum_fusion.6
  341.5 6.5 copy.53
  348.0 10.5 %fusion.427 = (f32[4,16,128]{2,1,0:T(8,128)S(1)}, f32[4,16,448,128]{3,2,1,0:T(8,128)}) fusion(bf16[4,448,16,64]{1,3,2,0:T(8,128)(2,1)} %bitcast.213, bf16[4,128,16,64]{1,3,2,0:T(8,128)(2,1)S(1)} %bitcast.221, pred[4,448,128]{2,1,0:T(8,128)(4,1)S(1)} %copy-done.20), kind=kOutput, calls=%fused_computation.522 | convolution fusion | flops 480763904 | bytes 19660800 | tf_op jit(solution)/shard_map/sqhe,skhe->shkq/dot_general | solution.py:96
  358.5 9.1 %fusion.1 = f32[4,16,128]{2,1,0:T(8,128)S(1)} fusion(f32[4,16,448,128]{3,2,1,0:T(8,128)} %get-tuple-element.61, f32[4,16,128]{2,1,0:T(8,128)S(1)} %get-tuple-element.60), kind=kLoop, calls=%fused_computation.19 | loop fusion | flops 7331840 | bytes 14745600 | tf_op jit(solution)/shard_map/reduce_sum | solution.py:113
  367.7 8.5 fusion.237
  380.3 10.4 %fusion.28 = f32[512,4096]{1,0:T(8,128)} fusion(bf16[1,4096,1024]{2,1,0:T(8,128)(2,1)} %all-gather.15.cloned.1.call-done, f32[512,1024]{1,0:T(8,128)S(1)} %get-tuple-element.63, f32[1024]{0:T(1024)S(1)} %bitcast.260, f32[1024]{0:T(1024)S(1)} %bitcast.257, f32[512]{0:T(512)S(1)} %fusion.283, f32[512]{0:T(512)S(1)} %broadcast_multiply_fusion.3), kind=kOutput, calls=%fused_computation.50 | convolution fusion | flops 4297588736 | bytes 18886656 | tf_op jit(solution)/shard_map/dot_general | solution.py:48
  390.7 26.6 %fusion.429 = (f32[512]{0:T(512)S(1)}, f32[512,1024]{1,0:T(8,128)S(1)}) fusion(f32[1024]{0:T(1024)S(1)} %bitcast.247, bf16[1,4096,1024]{2,1,0:T(8,128)(2,1)} %all-gather.17.cloned.1.call-done, f32[512,4096]{1,0:T(8,128)} %fusion.28, f32[4096]{0:T(1024)S(1)} %fusion.269, f32[1024]{0:T(1024)S(1)} %bitcast.261, f32[1024]{0:T(1024)S(1)} %bitcast.258, ...), kind=kOutput, calls=%fused_computation.524 | convolution fusion | flops 4437048832 | bytes 21006336 | tf_op jit(solution)/shard_map/dot_general | solution.py:44
  420.6 37.3 %multiply_reduce_fusion.4 = (f32[512]{0:T(512)S(1)}, f32[512,1024]{1,0:T(8,128)}) fusion(f32[512,1024]{1,0:T(8,128)S(1)} %get-tuple-element.63, f32[512]{0:T(512)S(1)} %broadcast_multiply_fusion.3, f32[1024]{0:T(1024)S(1)} %bitcast.259, bf16[1,4096,1024]{2,1,0:T(8,128)(2,1)} %all-gather.15.cloned.1.call-done, f32[512,4096]{1,0:T(8,128)} %fusion.28, ...), kind=kOutput, calls=%fused_computation.257 | convolution fusion | flops 8747220992 | bytes 31483904 | tf_op jit(solution)/shard_map/dot_general | solution.py:44
  467.6 11.9 %fusion.68 = f32[4,16,64,448]{3,2,1,0:T(8,128)} fusion(bf16[4,128,16,64]{1,3,2,0:T(8,128)(2,1)S(1)} %copy.58, f32[4,16,448,128]{3,2,1,0:T(8,128)} %get-tuple-element.61, f32[4,16,128]{2,1,0:T(8,128)S(1)} %copy-done.30), kind=kOutput, calls=%fused_computation.121 | convolution fusion | flops 477102080 | bytes 23101440 | tf_op jit(solution)/shard_map/shkq,sqhe->skhe/dot_general | solution.py:189
  479.5 10.2 %multiply_reduce_fusion.1 = (f32[4,16,128]{2,1,0:T(8,128)S(1)}, f32[4,16,448,128]{3,2,1,0:T(8,128)}) fusion(f32[4,16,448,128]{3,2,1,0:T(8,128)} %get-tuple-element.61, f32[4,16,128]{2,1,0:T(8,128)S(1)} %copy-done.30, bf16[4,448,16,64]{1,3,2,0:T(8,128)(2,1)S(1)} %bitcast.226, bf16[4,128,16,64]{1,3,2,0:T(8,128)(2,1)S(1)} %copy.58), kind=kOutput, calls=%fused_computation.10 | convolution fusion | flops 480763904 | bytes 34144256 | tf_op jit(solution)/shard_map/sqhe,skhe->shkq/dot_general | solution.py:176
  489.6 7.8 slice.247
  497.4 6.6 copy.81
  504.0 10.9 %multiply_convert_fusion.1 = bf16[4,16,448,128]{3,2,1,0:T(8,128)(2,1)S(1)} fusion(f32[4,16,448,128]{3,2,1,0:T(8,128)} %get-tuple-element.69, f32[4,16,448,128]{3,2,1,0:T(8,128)} %get-tuple-element.61, f32[4,16,128]{2,1,0:T(8,128)S(1)} %get-tuple-element.68, f32[4,16,128]{2,1,0:T(8,128)S(1)} %copy-done.30), kind=kLoop, calls=%fused_computation.9 | loop fusion | flops 14680064 | bytes 36765696 | tf_op jit(solution)/shard_map/convert_element_type | solution.py:180
  514.9 3.2 broadcast_multiply_fusion.1
  518.2 3.3 copy-done.2
  521.5 4.3 slice.246
  525.8 6.6 copy.80
  532.4 8.2 fusion.3
  540.7 4.9 fusion.414
  545.6 3.7 collective-permute-start.10
  550.6 35.2 %all-gather.5 = bf16[1,4096]{1,0:T(2,128)(2,1)S(1)} all-gather(bf16[1,512]{1,0:T(2,128)(2,1)S(1)} %copy-done.58), channel_id=7, replica_groups=mesh['rows'=4,'wide'=8] {'wide'}, dimensions={1}, use_global_device_ids=true | all-gather | bytes 9216 | tf_op jit(solution)/shard_map/all_gather | solution.py:160
  585.8 4.8 fusion.238
  593.9 4.1 fusion.95
  598.6 6.7 multiply_reduce_fusion.3
  607.3 37.1 %multiply_reduce_fusion.2 = (f32[512]{0:T(512)S(1)}, f32[512,1024]{1,0:T(8,128)}) fusion(f32[512,1024]{1,0:T(8,128)S(1)} %copy-done.14, f32[512]{0:T(512)S(1)} %copy-done.39, f32[1024]{0:T(1024)S(1)} %bitcast.253, bf16[1,4096,1024]{2,1,0:T(8,128)(2,1)} %all-gather.11.cloned.1.call-done, f32[512,4096]{1,0:T(8,128)} %fusion.36, f32[4096]{0:T(1024)S(1)} %bitcast.244, ...), kind=kOutput, calls=%fused_computation.252 | convolution fusion | flops 8747220992 | bytes 31483904 | tf_op jit(solution)/shard_map/dot_general | solution.py:44
  654.0 11.8 %fusion.66 = f32[4,16,64,448]{3,2,1,0:T(8,128)} fusion(bf16[4,128,16,64]{1,3,2,0:T(8,128)(2,1)S(1)} %copy.65, f32[4,16,448,128]{3,2,1,0:T(8,128)} %get-tuple-element.55, f32[4,16,128]{2,1,0:T(8,128)S(1)} %log_add_fusion), kind=kOutput, calls=%fused_computation.120 | convolution fusion | flops 477102080 | bytes 23101440 | tf_op jit(solution)/shard_map/shkq,sqhe->skhe/dot_general | solution.py:189
  665.8 10.1 %multiply_reduce_fusion = (f32[4,16,128]{2,1,0:T(8,128)S(1)}, f32[4,16,448,128]{3,2,1,0:T(8,128)}) fusion(f32[4,16,448,128]{3,2,1,0:T(8,128)} %get-tuple-element.55, f32[4,16,128]{2,1,0:T(8,128)S(1)} %log_add_fusion, bf16[4,448,16,64]{1,3,2,0:T(8,128)(2,1)S(1)} %bitcast.224, bf16[4,128,16,64]{1,3,2,0:T(8,128)(2,1)S(1)} %copy.65), kind=kOutput, calls=%fused_computation.7 | convolution fusion | flops 480763904 | bytes 34144256 | tf_op jit(solution)/shard_map/sqhe,skhe->shkq/dot_general | solution.py:176
  676.0 7.6 slice.253
  683.6 6.6 copy.83
  690.2 10.9 %multiply_convert_fusion = bf16[4,16,448,128]{3,2,1,0:T(8,128)(2,1)S(1)} fusion(f32[4,16,448,128]{3,2,1,0:T(8,128)} %get-tuple-element.75, f32[4,16,448,128]{3,2,1,0:T(8,128)} %get-tuple-element.55, f32[4,16,128]{2,1,0:T(8,128)S(1)} %get-tuple-element.74, f32[4,16,128]{2,1,0:T(8,128)S(1)} %log_add_fusion), kind=kLoop, calls=%fused_computation.6 | loop fusion | flops 14680064 | bytes 36765696 | tf_op jit(solution)/shard_map/convert_element_type | solution.py:180
  701.2 3.2 broadcast_multiply_fusion
  704.4 3.3 copy-done.3
  707.7 4.4 slice.252
  712.1 6.6 copy.82
  718.6 8.3 fusion.2
  726.9 5.0 fusion.413
  731.9 3.6 collective-permute-start.12
  745.6 6.0 fusion.239
  754.9 125.5 %all-reduce.4.cloned.1.call-done = f32[2,2,64,1024]{2,3,1,0:T(8,128)} async-done(((f32[2,2,64,1024]{2,3,1,0:T(8,128)}), f32[2,2,64,1024]{2,3,1,0:T(8,128)}) %all-reduce.4.cloned.1.call-update) | async-done | bytes 1048592 | tf_op jit(solution)/shard_map/psum | solution.py:219
  880.4 3.1 copy.71
  883.5 4.0 fusion.91
  887.6 7.5 add_add_fusion.8
  (262 shorter events, 85.3 us)
Async XLA Ops:
  7.2 170.2 %all-gather.11.cloned.1.call-start = ((), (), s32[]{:S(2)}) async-start(), calls=%async_computation.1 | async-start | bytes 9437184 | tf_op jit(solution)/shard_map/all_gather | solution.py:124
  10.4 190.9 %all-gather.13.cloned.1.call-start = ((), (), s32[]{:S(2)}) async-start(), calls=%async_computation.2 | async-start | bytes 9437184 | tf_op jit(solution)/shard_map/all_gather | solution.py:125
  13.5 366.8 %all-gather.15.cloned.1.call-start = ((), (), s32[]{:S(2)}) async-start(), calls=%async_computation.3 | async-start | bytes 9437184 | tf_op jit(solution)/shard_map/all_gather | solution.py:124
  14.2 376.5 %all-gather.17.cloned.1.call-start = ((), (), s32[]{:S(2)}) async-start(), calls=%async_computation.4 | async-start | bytes 9437184 | tf_op jit(solution)/shard_map/all_gather | solution.py:125
  14.9 14.0 %copy-start.62 = (bf16[2,512]{1,0:T(2,128)(2,1)S(1)}, bf16[2,512]{1,0:T(2,128)(2,1)}, u32[]{:S(2)}) copy-start(bf16[2,512]{1,0:T(2,128)(2,1)} %param.25) | copy-start | bytes 6148
  14.9 19.1 %copy-start.37 = (s32[4,1024]{1,0:T(4,128)S(1)}, s32[4,1024]{1,0:T(4,128)}, u32[]{:S(2)}) copy-start(s32[4,1024]{1,0:T(4,128)} %param.17) | copy-start | bytes 49156
  14.9 19.2 %copy-start.49 = (f32[2,2,1024]{2,1,0:T(2,128)S(1)}, f32[2,2,1024]{2,1,0:T(2,128)}, u32[]{:S(2)}) copy-start(f32[2,2,1024]{2,1,0:T(2,128)} %param.22) | copy-start | bytes 49156
  14.9 20.8 %copy-start.26 = (bf16[2,2,64,1024]{3,2,1,0:T(8,128)(2,1)S(1)}, bf16[2,2,64,1024]{3,2,1,0:T(8,128)(2,1)}, u32[]{:S(2)}) copy-start(bf16[2,2,64,1024]{3,2,1,0:T(8,128)(2,1)} %param.28) | copy-start | bytes 1572868
  14.9 21.5 %copy-start.50 = (f32[2,2,1024]{2,1,0:T(2,128)S(1)}, f32[2,2,1024]{2,1,0:T(2,128)}, u32[]{:S(2)}) copy-start(f32[2,2,1024]{2,1,0:T(2,128)} %param.23) | copy-start | bytes 49156
  14.9 83.8 %copy-start.60 = (f32[2,1024]{1,0:T(2,128)S(1)}, f32[2,1024]{1,0:T(2,128)}, u32[]{:S(2)}) copy-start(f32[2,1024]{1,0:T(2,128)} %param.21) | copy-start | bytes 24580
  14.9 103.9 %copy-start.61 = (f32[2,1024]{1,0:T(2,128)S(1)}, f32[2,1024]{1,0:T(2,128)}, u32[]{:S(2)}) copy-start(f32[2,1024]{1,0:T(2,128)} %param.27) | copy-start | bytes 24580
  23.1 101.7 %collective-permute-start.1 = (bf16[4,128,2048]{2,1,0:T(8,128)(2,1)S(1)}, bf16[4,128,2048]{2,1,0:T(8,128)(2,1)}, u32[]{:S(2)}, u32[]{:S(2)}) collective-permute-start(bf16[4,128,2048]{2,1,0:T(8,128)(2,1)S(1)} %slice.238), channel_id=1, source_target_pairs={{1,0},{2,1},{3,2},{4,3},{5,4},{6,5},{7,6},{9,8},{10,9},{11,10},{12... | collective-permute-start | bytes 6291464 | tf_op jit(solution)/shard_map/ppermute | solution.py:20
  24.4 100.4 %collective-permute-start = (bf16[4,128,2048]{2,1,0:T(8,128)(2,1)S(1)}, bf16[4,128,2048]{2,1,0:T(8,128)(2,1)}, u32[]{:S(2)}, u32[]{:S(2)}) collective-permute-start(bf16[4,128,2048]{2,1,0:T(8,128)(2,1)S(1)} %slice.238), channel_id=1, source_target_pairs={{0,1},{1,2},{2,3},{3,4},{4,5},{5,6},{6,7},{8,9},{9,10},{10,11},{11... | collective-permute-start | bytes 6291464 | tf_op jit(solution)/shard_map/ppermute | solution.py:17
  29.9 7.1 collective-permute-start.2
  33.9 846.4 %all-reduce.4.cloned.1.call-start = ((), (), s32[]{:S(2)}) async-start(), calls=%async_computation | async-start | bytes 4194304 | tf_op jit(solution)/shard_map/psum | solution.py:219
  34.7 166.6 %copy-start.65 = (f32[1,1,1024]{2,1,0:T(1,128)}, f32[1,1,1024]{2,1,0:T(1,128)S(1)}, u32[]{:S(2)}) copy-start(f32[1,1,1024]{2,1,0:T(1,128)S(1)} %get-tuple-element.40) | copy-start | bytes 12292
  37.1 78.2 %collective-permute-start.3 = (bf16[1024]{0:T(1024)(128)(2,1)S(1)}, bf16[1024]{0:T(1024)(128)(2,1)S(1)}, u32[]{:S(2)}, u32[]{:S(2)}) collective-permute-start(bf16[1024]{0:T(1024)(128)(2,1)S(1)} %pad_maximum_fusion.17), channel_id=1, source_target_pairs={{0,6},{1,7},{2,0},{3,1},{4,2},{5,3},{6,4},{7,5},{8,14},{9,15},{10,... | collective-permute-start | bytes 6152 | tf_op jit(solution)/shard_map/ppermute | solution.py:134
  115.2 9.4 %collective-permute-start.4 = (bf16[2048]{0:T(1024)(128)(2,1)S(1)}, bf16[2048]{0:T(1024)(128)(2,1)S(1)}, u32[]{:S(2)}, u32[]{:S(2)}) collective-permute-start(bf16[2048]{0:T(1024)(128)(2,1)S(1)} %pad_maximum_fusion.15), channel_id=1, source_target_pairs={{0,4},{1,5},{2,6},{3,7},{4,0},{5,1},{6,2},{7,3},{8,12},{9,13},{10,... | collective-permute-start | bytes 12296 | tf_op jit(solution)/shard_map/ppermute | solution.py:134
  123.4 22.3 %copy-start.5 = (bf16[4,128,1024]{1,2,0:T(8,128)(2,1)}, bf16[4,128,1024]{1,2,0:T(8,128)(2,1)S(1)}, u32[]{:S(2)}) copy-start(bf16[4,128,1024]{1,2,0:T(8,128)(2,1)S(1)} %copy.51) | copy-start | bytes 3145732
  124.6 21.1 %copy-start.19 = (pred[4,448,128]{2,1,0:T(8,128)(4,1)}, pred[4,448,128]{2,1,0:T(8,128)(4,1)S(1)}, u32[]{:S(2)}) copy-start(pred[4,448,128]{2,1,0:T(8,128)(4,1)S(1)} %concatenate.84) | copy-start | bytes 688132
  156.2 17.6 %copy-start.31 = (f32[4,16,128]{2,1,0:T(8,128)}, f32[4,16,128]{2,1,0:T(8,128)S(1)}, u32[]{:S(2)}) copy-start(f32[4,16,128]{2,1,0:T(8,128)S(1)} %get-tuple-element.54) | copy-start | bytes 98308
  156.3 9.0 copy-start.9
  165.2 9.5 %copy-start.72 = (bf16[2,1024,1024]{2,1,0:T(8,128)(2,1)S(1)}, bf16[2,1024,1024]{2,1,0:T(8,128)(2,1)}, u32[]{:S(2)}) copy-start(bf16[2,1024,1024]{2,1,0:T(8,128)(2,1)} %param.20) | copy-start | bytes 12582916
  165.2 9.5 %copy-start.75 = (bf16[4,128,1024]{2,1,0:T(8,128)(2,1)S(1)}, bf16[4,128,1024]{2,1,0:T(8,128)(2,1)}, u32[]{:S(2)}) copy-start(bf16[4,128,1024]{2,1,0:T(8,128)(2,1)} %param.16) | copy-start | bytes 3145732
  176.2 25.1 %copy-start.13 = (f32[512,1024]{1,0:T(8,128)}, f32[512,1024]{1,0:T(8,128)S(1)}, u32[]{:S(2)}) copy-start(f32[512,1024]{1,0:T(8,128)S(1)} %get-tuple-element.57) | copy-start | bytes 6291460
  176.2 25.1 %copy-start.38 = (f32[512]{0:T(512)}, f32[512]{0:T(512)S(1)}, u32[]{:S(2)}) copy-start(f32[512]{0:T(512)S(1)} %broadcast_multiply_fusion.5) | copy-start | bytes 6148
  177.4 23.9 %copy-start.54 = (f32[512]{0:T(512)}, f32[512]{0:T(512)S(1)}, u32[]{:S(2)}) copy-start(f32[512]{0:T(512)S(1)} %fusion.281) | copy-start | bytes 6148
  201.3 27.6 %copy-start.53 = (f32[1,3072]{1,0:T(1,128)S(1)}, f32[1,3072]{1,0:T(1,128)}, u32[]{:S(2)}) copy-start(f32[1,3072]{1,0:T(1,128)} %get-tuple-element.36) | copy-start | bytes 36868
  201.3 27.6 %copy-start.67 = (f32[1,1,1024]{2,1,0:T(1,128)S(1)}, f32[1,1,1024]{2,1,0:T(1,128)}, u32[]{:S(2)}) copy-start(f32[1,1,1024]{2,1,0:T(1,128)} %get-tuple-element.39) | copy-start | bytes 12292
  201.3 27.6 %copy-start.71 = (f32[1,1,1024]{2,1,0:T(1,128)S(1)}, f32[1,1,1024]{2,1,0:T(1,128)}, u32[]{:S(2)}) copy-start(f32[1,1,1024]{2,1,0:T(1,128)} %get-tuple-element.43) | copy-start | bytes 12292
  227.7 149.4 %copy-start.40 = (f32[512]{0:T(512)}, f32[512]{0:T(512)S(1)}, u32[]{:S(2)}) copy-start(f32[512]{0:T(512)S(1)} %broadcast_multiply_fusion.4) | copy-start | bytes 6148
  228.0 149.1 %copy-start.56 = (f32[512]{0:T(512)}, f32[512]{0:T(512)S(1)}, u32[]{:S(2)}) copy-start(f32[512]{0:T(512)S(1)} %fusion.282) | copy-start | bytes 6148
  228.9 12.6 %copy-start.52 = (bf16[512]{0:T(512)(128)(2,1)S(1)}, bf16[512]{0:T(512)(128)(2,1)}, u32[]{:S(2)}) copy-start(bf16[512]{0:T(512)(128)(2,1)} %get-tuple-element.9) | copy-start | bytes 3076
  228.9 77.2 %copy-start.59 = (bf16[1,512]{1,0:T(2,128)(2,1)S(1)}, bf16[1,512]{1,0:T(2,128)(2,1)}, u32[]{:S(2)}) copy-start(bf16[1,512]{1,0:T(2,128)(2,1)} %get-tuple-element.51) | copy-start | bytes 3076
  235.8 86.8 %collective-permute-start.6 = (bf16[4,128,2048]{2,1,0:T(8,128)(2,1)S(1)}, bf16[4,128,2048]{2,1,0:T(8,128)(2,1)}, u32[]{:S(2)}, u32[]{:S(2)}) collective-permute-start(bf16[4,128,2048]{2,1,0:T(8,128)(2,1)S(1)} %slice.242), channel_id=1, source_target_pairs={{1,0},{2,1},{3,2},{4,3},{5,4},{6,5},{7,6},{9,8},{10,9},{11,10},{12... | collective-permute-start | bytes 6291464 | tf_op jit(solution)/shard_map/ppermute | solution.py:20
  237.1 85.5 %collective-permute-start.5 = (bf16[4,128,2048]{2,1,0:T(8,128)(2,1)S(1)}, bf16[4,128,2048]{2,1,0:T(8,128)(2,1)}, u32[]{:S(2)}, u32[]{:S(2)}) collective-permute-start(bf16[4,128,2048]{2,1,0:T(8,128)(2,1)S(1)} %slice.242), channel_id=1, source_target_pairs={{0,1},{1,2},{2,3},{3,4},{4,5},{5,6},{6,7},{8,9},{9,10},{10,11},{11... | collective-permute-start | bytes 6291464 | tf_op jit(solution)/shard_map/ppermute | solution.py:17
  241.5 1.3 collective-permute-start.7
  242.8 61.3 %collective-permute-start.8 = (bf16[1024]{0:T(1024)(128)(2,1)S(1)}, bf16[1024]{0:T(1024)(128)(2,1)S(1)}, u32[]{:S(2)}, u32[]{:S(2)}) collective-permute-start(bf16[1024]{0:T(1024)(128)(2,1)S(1)} %pad_maximum_fusion.18), channel_id=1, source_target_pairs={{0,6},{1,7},{2,0},{3,1},{4,2},{5,3},{6,4},{7,5},{8,14},{9,15},{10,... | collective-permute-start | bytes 6152 | tf_op jit(solution)/shard_map/ppermute | solution.py:134
  304.1 15.7 %collective-permute-start.9 = (bf16[2048]{0:T(1024)(128)(2,1)S(1)}, bf16[2048]{0:T(1024)(128)(2,1)S(1)}, u32[]{:S(2)}, u32[]{:S(2)}) collective-permute-start(bf16[2048]{0:T(1024)(128)(2,1)S(1)} %pad_maximum_fusion.16), channel_id=1, source_target_pairs={{0,4},{1,5},{2,6},{3,7},{4,0},{5,1},{6,2},{7,3},{8,12},{9,13},{10,... | collective-permute-start | bytes 12296 | tf_op jit(solution)/shard_map/ppermute | solution.py:134
  322.6 25.4 %copy-start.7 = (bf16[4,128,1024]{1,2,0:T(8,128)(2,1)}, bf16[4,128,1024]{1,2,0:T(8,128)(2,1)S(1)}, u32[]{:S(2)}) copy-start(bf16[4,128,1024]{1,2,0:T(8,128)(2,1)S(1)} %copy.55) | copy-start | bytes 3145732
  337.3 10.7 %copy-start.20 = (pred[4,448,128]{2,1,0:T(8,128)(4,1)S(1)}, pred[4,448,128]{2,1,0:T(8,128)(4,1)}, u32[]{:S(2)}) copy-start(pred[4,448,128]{2,1,0:T(8,128)(4,1)} %copy-done.19) | copy-start | bytes 688132
  358.5 9.2 %copy-start.11 = (bf16[4,448,1024]{1,2,0:T(8,128)(2,1)S(1)}, bf16[4,448,1024]{1,2,0:T(8,128)(2,1)}, u32[]{:S(2)}) copy-start(bf16[4,448,1024]{1,2,0:T(8,128)(2,1)} %copy.53) | copy-start | bytes 11010052
  367.7 9.4 %copy-start.16 = (f32[512,1024]{1,0:T(8,128)S(1)}, f32[512,1024]{1,0:T(8,128)}, u32[]{:S(2)}) copy-start(f32[512,1024]{1,0:T(8,128)} %copy-done.15) | copy-start | bytes 6291460
  367.7 9.4 %copy-start.64 = (f32[1,1024]{1,0:T(1,128)S(1)}, f32[1,1024]{1,0:T(1,128)}, u32[]{:S(2)}) copy-start(f32[1,1024]{1,0:T(1,128)} %get-tuple-element.48) | copy-start | bytes 12292
  367.7 9.4 %copy-start.73 = (bf16[2,1024,1024]{2,1,0:T(8,128)(2,1)S(1)}, bf16[2,1024,1024]{2,1,0:T(8,128)(2,1)}, u32[]{:S(2)}) copy-start(bf16[2,1024,1024]{2,1,0:T(8,128)(2,1)} %param.20) | copy-start | bytes 12582916
  380.3 10.4 %copy-start.63 = (f32[1,1024]{1,0:T(1,128)S(1)}, f32[1,1024]{1,0:T(1,128)}, u32[]{:S(2)}) copy-start(f32[1,1024]{1,0:T(1,128)} %get-tuple-element.46) | copy-start | bytes 12292
  390.7 26.6 %copy-start.18 = (bf16[4,128,1024]{2,1,0:T(8,128)(2,1)S(1)}, bf16[4,128,1024]{2,1,0:T(8,128)(2,1)}, u32[]{:S(2)}) copy-start(bf16[4,128,1024]{2,1,0:T(8,128)(2,1)} %param.29) | copy-start | bytes 3145732
  390.7 26.6 %copy-start.35 = (f32[1,1,1024]{2,1,0:T(1,128)S(1)}, f32[1,1,1024]{2,1,0:T(1,128)}, u32[]{:S(2)}) copy-start(f32[1,1,1024]{2,1,0:T(1,128)} %get-tuple-element.38) | copy-start | bytes 12292
  390.7 27.4 %copy-start.48 = (f32[1,1,1024]{2,1,0:T(1,128)S(1)}, f32[1,1,1024]{2,1,0:T(1,128)}, u32[]{:S(2)}) copy-start(f32[1,1,1024]{2,1,0:T(1,128)} %get-tuple-element.42) | copy-start | bytes 12292
  420.6 37.3 %copy-start.47 = (f32[512]{0:T(512)S(1)}, f32[512]{0:T(512)}, u32[]{:S(2)}) copy-start(f32[512]{0:T(512)} %copy-done.46) | copy-start | bytes 6148
  467.5 11.9 %copy-start.12 = (bf16[4,448,1024]{1,2,0:T(8,128)(2,1)S(1)}, bf16[4,448,1024]{1,2,0:T(8,128)(2,1)}, u32[]{:S(2)}) copy-start(bf16[4,448,1024]{1,2,0:T(8,128)(2,1)} %copy.53) | copy-start | bytes 11010052
  504.0 10.9 %copy-start.8 = (bf16[4,128,1024]{1,2,0:T(8,128)(2,1)S(1)}, bf16[4,128,1024]{1,2,0:T(8,128)(2,1)}, u32[]{:S(2)}) copy-start(bf16[4,128,1024]{1,2,0:T(8,128)(2,1)} %copy-done.7) | copy-start | bytes 3145732
  540.6 9.9 %copy-start.58 = (bf16[1,512]{1,0:T(2,128)(2,1)S(1)}, bf16[1,512]{1,0:T(2,128)(2,1)}, u32[]{:S(2)}) copy-start(bf16[1,512]{1,0:T(2,128)(2,1)} %get-tuple-element.50) | copy-start | bytes 3076
  540.6 45.1 %copy-start.32 = (f32[4,16,128]{2,1,0:T(8,128)S(1)}, f32[4,16,128]{2,1,0:T(8,128)}, u32[]{:S(2)}) copy-start(f32[4,16,128]{2,1,0:T(8,128)} %copy-done.31) | copy-start | bytes 98308
  540.6 45.2 %copy-start.34 = (f32[4,16,128]{2,1,0:T(8,128)S(1)}, f32[4,16,128]{2,1,0:T(8,128)}, u32[]{:S(2)}) copy-start(f32[4,16,128]{2,1,0:T(8,128)} %copy-done.33) | copy-start | bytes 98308
  540.6 45.2 %copy-start.4 = (bf16[4,448,1024]{1,2,0:T(8,128)(2,1)S(1)}, bf16[4,448,1024]{1,2,0:T(8,128)(2,1)}, u32[]{:S(2)}) copy-start(bf16[4,448,1024]{1,2,0:T(8,128)(2,1)} %copy.54) | copy-start | bytes 11010052
  545.6 48.3 %collective-permute-start.10 = (bf16[4,128,2048]{2,1,0:T(8,128)(2,1)}, bf16[4,128,2048]{2,1,0:T(8,128)(2,1)}, u32[]{:S(2)}, u32[]{:S(2)}) collective-permute-start(bf16[4,128,2048]{2,1,0:T(8,128)(2,1)} %get-tuple-element.21), channel_id=1, source_target_pairs={{0,1},{1,2},{2,3},{3,4},{4,5},{5,6},{6,7},{8,9},{9,10},{10,11},{11... | collective-permute-start | bytes 6291464 | tf_op jit(solution)/shard_map/ppermute | solution.py:17
  549.3 44.6 %collective-permute-start.11 = (bf16[4,128,2048]{2,1,0:T(8,128)(2,1)}, bf16[4,128,2048]{2,1,0:T(8,128)(2,1)}, u32[]{:S(2)}, u32[]{:S(2)}) collective-permute-start(bf16[4,128,2048]{2,1,0:T(8,128)(2,1)} %get-tuple-element.22), channel_id=1, source_target_pairs={{1,0},{2,1},{3,2},{4,3},{5,4},{6,5},{7,6},{9,8},{10,9},{11,10},{12... | collective-permute-start | bytes 6291464 | tf_op jit(solution)/shard_map/ppermute | solution.py:20
  607.3 37.2 %copy-start.43 = (f32[512]{0:T(512)S(1)}, f32[512]{0:T(512)}, u32[]{:S(2)}) copy-start(f32[512]{0:T(512)} %copy-done.42) | copy-start | bytes 6148
  607.3 37.2 %copy-start.55 = (f32[512]{0:T(512)S(1)}, f32[512]{0:T(512)}, u32[]{:S(2)}) copy-start(f32[512]{0:T(512)} %copy-done.54) | copy-start | bytes 6148
  654.0 11.8 %copy-start.10 = (bf16[4,448,1024]{1,2,0:T(8,128)(2,1)S(1)}, bf16[4,448,1024]{1,2,0:T(8,128)(2,1)}, u32[]{:S(2)}) copy-start(bf16[4,448,1024]{1,2,0:T(8,128)(2,1)} %copy.49) | copy-start | bytes 11010052
  690.2 10.9 %copy-start.6 = (bf16[4,128,1024]{1,2,0:T(8,128)(2,1)S(1)}, bf16[4,128,1024]{1,2,0:T(8,128)(2,1)}, u32[]{:S(2)}) copy-start(bf16[4,128,1024]{1,2,0:T(8,128)(2,1)} %copy-done.5) | copy-start | bytes 3145732
  731.9 151.7 %collective-permute-start.12 = (bf16[4,128,2048]{2,1,0:T(8,128)(2,1)}, bf16[4,128,2048]{2,1,0:T(8,128)(2,1)}, u32[]{:S(2)}, u32[]{:S(2)}) collective-permute-start(bf16[4,128,2048]{2,1,0:T(8,128)(2,1)} %get-tuple-element.19), channel_id=1, source_target_pairs={{0,1},{1,2},{2,3},{3,4},{4,5},{5,6},{6,7},{8,9},{9,10},{10,11},{11... | collective-permute-start | bytes 6291464 | tf_op jit(solution)/shard_map/ppermute | solution.py:17
  735.5 148.1 %collective-permute-start.13 = (bf16[4,128,2048]{2,1,0:T(8,128)(2,1)}, bf16[4,128,2048]{2,1,0:T(8,128)(2,1)}, u32[]{:S(2)}, u32[]{:S(2)}) collective-permute-start(bf16[4,128,2048]{2,1,0:T(8,128)(2,1)} %get-tuple-element.20), channel_id=1, source_target_pairs={{1,0},{2,1},{3,2},{4,3},{5,4},{6,5},{7,6},{9,8},{10,9},{11,10},{12... | collective-permute-start | bytes 6291464 | tf_op jit(solution)/shard_map/ppermute | solution.py:20
  (31 other events, 142.0 us)
Sparse Core Ops, SparseCore 0:
  10.5 101.7 all-gather.10
  114.4 85.6 all-gather.12
  201.8 93.0 all-gather.14
  296.9 87.7 all-gather.16
  745.7 134.6 all-reduce.3
